TPU v7x, 32 devices: a whole 2x2x4 slice. The times are simulated.
32 devices in a mesh: row: 4 (over z), col: 4 (over y, core), rep: 2 (over x).
Axes of the slice: x: 2, y: 2, z: 4, core: 2. Of those that a mesh axis runs over, the one named last changes fastest.
Arguments:
- amplitudes: bfloat16 [1024, 8192], P('row', 'col'), may hold values from -6 to 6
- intermediate: bfloat16 [8192, 1024], P('row', 'col'), may hold values from -0.0625 to 0.0625
Outputs:
- residual: float32 [8, 4, 32, 1024], P(None, 'col', None, ('row', 'rep'))
All inputs are finite; a program needn't handle non-finite values.
Results may differ from a plain program's by a relative error of at most 0.0029.
Values may be sent and summed in bfloat16 or wider, within the bound.
A program may use at most 128 MiB of HBM per device.

v0:
```python
import jax
import jax.numpy as jnp
from jax import lax
from jax.sharding import PartitionSpec as P


def local(amplitudes, intermediate):
    rows_axis = lax.axis_size("row")
    cols_axis = lax.axis_size("col")
    depth_axis = lax.axis_size("rep")
    layer_index = lax.axis_index("rep")
    owner_rows = rows_axis * depth_axis
    fold_count = owner_rows // cols_axis
    local_rows = amplitudes.shape[0]
    band_rows = local_rows // depth_axis
    local_cols = intermediate.shape[1]
    slice_width = local_cols // owner_rows
    own_rows = lax.dynamic_slice_in_dim(amplitudes, layer_index * band_rows, band_rows, 0)
    all_weights = lax.all_gather(intermediate, "row", axis=0, tiled=True)
    summed = jnp.dot(
        lax.all_gather(own_rows, "col", axis=1, tiled=True),
        all_weights,
        preferred_element_type=jnp.float32,
    )
    cycle = summed.astype(jnp.bfloat16)
    spread_block = cycle.reshape(band_rows, fold_count, cols_axis, slice_width)
    direct = lax.all_to_all(spread_block, "col", split_axis=2, concat_axis=1, tiled=True).reshape(
        band_rows, owner_rows, slice_width
    )
    stacked = cycle.reshape(cols_axis, slice_width, fold_count, cols_axis * slice_width)
    mirror = lax.all_to_all(
        lax.all_to_all(stacked, "col", split_axis=0, concat_axis=2, tiled=True),
        ("row", "rep"),
        split_axis=2,
        concat_axis=0,
        tiled=True,
    )
    mirror_part = mirror.reshape(owner_rows, slice_width, band_rows).astype(jnp.float32)
    direct_part = jnp.transpose(direct, (1, 2, 0)).astype(jnp.float32)
    return (mirror_part + direct_part).reshape(owner_rows, 1, slice_width, band_rows)


def solution(mesh):
    in_specs = (P("row", "col"), P("row", "col"))
    out_specs = P(None, "col", None, ("row", "rep"))
    return jax.shard_map(local, mesh=mesh, in_specs=in_specs, out_specs=out_specs, check_vma=False)
```

profile of v0, /device:TPU:0, one launch (start us, length us, event | category | flops | bytes accessed | tf_op | source)
XLA Modules:
  0.0 153.2 jit_solution(1492077100807773133)
XLA Ops:
  6.5 0.0 copy-start
  6.5 0.0 all-gather.3.cloned.1.call-start
  6.5 1.2 copy-done
  7.8 0.9 constant_dynamic-slice_fusion
  8.6 0.0 all-gather.3.cloned.1.call-update
  8.6 0.0 all-gather.5.cloned.1.call-start
  8.7 0.7 all-gather.5.cloned.1.call-update
  9.4 24.8 %all-gather.3.cloned.1.call-done = bf16[128,8192]{1,0:T(8,128)(2,1)} async-done(((bf16[128,2048]{1,0:T(8,128)(2,1)}), bf16[128,8192]{1,0:T(8,128)(2,1)}) %all-gather.3.cloned.1.call-update) | async-done | bytes 2097168 | tf_op jit(solution)/shard_map/all_gather | solution.py:21
  34.2 82.3 %all-gather.5.cloned.1.call-done = bf16[8192,256]{1,0:T(8,128)(2,1)} async-done(((bf16[2048,256]{1,0:T(8,128)(2,1)}), bf16[8192,256]{1,0:T(8,128)(2,1)}) %all-gather.5.cloned.1.call-update) | async-done | bytes 4194320 | tf_op jit(solution)/shard_map/all_gather | solution.py:19
  116.6 3.5 %convolution_convert_fusion = bf16[128,256]{1,0:T(8,128)(2,1)S(1)} fusion(bf16[128,8192]{1,0:T(8,128)(2,1)} %all-gather.3.cloned.1.call-done, bf16[8192,256]{1,0:T(8,128)(2,1)} %all-gather.5.cloned.1.call-done), kind=kOutput, calls=%fused_computation | convolution fusion | flops 536903680 | bytes 6356992 | tf_op jit(solution)/shard_map/dot_general | solution.py:20
  120.1 0.7 reshape.21
  120.7 3.3 %all-to-all-start = ((bf16[4,32,2,128]{3,2,1,0:T(2,128)(2,1)}), bf16[4,32,2,128]{3,2,1,0:T(2,128)(2,1)S(1)}, u32[]{:S(2)}, u32[]{:S(2)}) async-start(bf16[4,32,2,128]{3,2,1,0:T(2,128)(2,1)} %reshape.21), calls=%async_computation | async-start | bytes 131072 | tf_op jit(solution)/shard_map/all_to_all | solution.py:32
  124.0 0.1 copy.13
  124.2 0.6 copy.14
  124.8 3.3 %all-to-all-done = bf16[4,32,2,128]{3,2,1,0:T(2,128)(2,1)S(1)} async-done(((bf16[4,32,2,128]{3,2,1,0:T(2,128)(2,1)}), bf16[4,32,2,128]{3,2,1,0:T(2,128)(2,1)S(1)}, u32[]{:S(2)}, u32[]{:S(2)}) %all-to-all-start) | async-done | bytes 65568 | tf_op jit(solution)/shard_map/all_to_all | solution.py:32
  128.1 3.3 %all-to-all-start.2 = ((bf16[128,2,4,32]{0,3,1,2:T(8,128)(2,1)}), bf16[128,2,4,32]{0,3,1,2:T(8,128)(2,1)S(1)}, u32[]{:S(2)}, u32[]{:S(2)}) async-start(bf16[128,2,4,32]{0,3,1,2:T(8,128)(2,1)} %copy.14), calls=%async_computation.2 | async-start | bytes 131072 | tf_op jit(solution)/shard_map/all_to_all | solution.py:27
  131.4 0.6 copy.11
  132.1 3.4 %all-to-all-done.2 = bf16[128,2,4,32]{0,3,1,2:T(8,128)(2,1)S(1)} async-done(((bf16[128,2,4,32]{0,3,1,2:T(8,128)(2,1)}), bf16[128,2,4,32]{0,3,1,2:T(8,128)(2,1)S(1)}, u32[]{:S(2)}, u32[]{:S(2)}) %all-to-all-start.2) | async-done | bytes 65568 | tf_op jit(solution)/shard_map/all_to_all | solution.py:27
  135.5 3.3 %all-to-all-start.1 = ((bf16[1,32,8,128]{3,1,0,2:T(8,128)(2,1)}), bf16[1,32,8,128]{3,1,0,2:T(8,128)(2,1)S(1)}, u32[]{:S(2)}, u32[]{:S(2)}) async-start(bf16[1,32,8,128]{3,1,0,2:T(8,128)(2,1)} %bitcast.2), calls=%async_computation.1 | async-start | bytes 131072 | tf_op jit(solution)/shard_map/all_to_all | solution.py:31
  138.9 6.8 %all-to-all-done.1 = bf16[1,32,8,128]{3,1,0,2:T(8,128)(2,1)S(1)} async-done(((bf16[1,32,8,128]{3,1,0,2:T(8,128)(2,1)}), bf16[1,32,8,128]{3,1,0,2:T(8,128)(2,1)S(1)}, u32[]{:S(2)}, u32[]{:S(2)}) %all-to-all-start.1) | async-done | bytes 65568 | tf_op jit(solution)/shard_map/all_to_all | solution.py:31
  145.7 0.7 bitcast_add_fusion
  (1 shorter events, 0.0 us)
Async XLA Ops:
  6.5 1.2 copy-start
  6.5 27.7 %all-gather.3.cloned.1.call-start = ((), (), s32[]{:S(2)}) async-start(), calls=%async_computation.3 | async-start | bytes 2621440 | tf_op jit(solution)/shard_map/all_gather | solution.py:21
  8.6 107.9 %all-gather.5.cloned.1.call-start = ((), (), s32[]{:S(2)}) async-start(), calls=%async_computation.4 | async-start | bytes 5242880 | tf_op jit(solution)/shard_map/all_gather | solution.py:19
  120.7 7.4 %all-to-all-start = ((bf16[4,32,2,128]{3,2,1,0:T(2,128)(2,1)}), bf16[4,32,2,128]{3,2,1,0:T(2,128)(2,1)S(1)}, u32[]{:S(2)}, u32[]{:S(2)}) async-start(bf16[4,32,2,128]{3,2,1,0:T(2,128)(2,1)} %reshape.21), calls=%async_computation | async-start | bytes 131072 | tf_op jit(solution)/shard_map/all_to_all | solution.py:32
  128.1 7.4 %all-to-all-start.2 = ((bf16[128,2,4,32]{0,3,1,2:T(8,128)(2,1)}), bf16[128,2,4,32]{0,3,1,2:T(8,128)(2,1)S(1)}, u32[]{:S(2)}, u32[]{:S(2)}) async-start(bf16[128,2,4,32]{0,3,1,2:T(8,128)(2,1)} %copy.14), calls=%async_computation.2 | async-start | bytes 131072 | tf_op jit(solution)/shard_map/all_to_all | solution.py:27
  135.5 10.2 %all-to-all-start.1 = ((bf16[1,32,8,128]{3,1,0,2:T(8,128)(2,1)}), bf16[1,32,8,128]{3,1,0,2:T(8,128)(2,1)S(1)}, u32[]{:S(2)}, u32[]{:S(2)}) async-start(bf16[1,32,8,128]{3,1,0,2:T(8,128)(2,1)} %bitcast.2), calls=%async_computation.1 | async-start | bytes 131072 | tf_op jit(solution)/shard_map/all_to_all | solution.py:31
Sparse Core Ops, SparseCore 0:
  8.9 25.2 all-gather.2
  35.8 80.7 all-gather.4
where the time goes:
time: 154 us; the launch traced here: 153 us
  waiting for transfers between devices  121 us (79%)
  between operations  13.4 us (9%)
  starting transfers between devices  9.96 us (6%)
  local copies, waits for them, and re-layouts  4.12 us (3%)
  matrix products  3.53 us (2%)
    all_gather x1, waiting for transfers between devices, local(): all_weights = lax.all_gather(intermediate, 'row', axis=0, tiled=True)  82.3 us
    all_gather x1, waiting for transfers between devices, local(): lax.all_gather(own_rows, 'col', axis=1, tiled=True)  24.8 us
    all_to_all x1, waiting for transfers between devices, local(): lax.all_to_all(lax.all_to_all(stacked, 'col', split_axis=0, concat_axis=2...  6.82 us
    dot_general x1, matrix products, local(): jnp.dot(lax.all_gather(own_rows, 'col', axis=1, tiled=True), all_weights,...  3.53 us
    all_to_all x1, waiting for transfers between devices, local(): lax.all_to_all(spread_block, 'col', split_axis=2, concat_axis=1, tiled=True)  3.44 us
    all_to_all x1, starting transfers between devices, local(): lax.all_to_all(lax.all_to_all(stacked, 'col', split_axis=0, concat_axis=2...  3.35 us
    all_to_all x1, waiting for transfers between devices, local(): lax.all_to_all(stacked, 'col', split_axis=0, concat_axis=2, tiled=True)  3.33 us
    all_to_all x1, starting transfers between devices, local(): lax.all_to_all(spread_block, 'col', split_axis=2, concat_axis=1, tiled=True)  3.29 us
  transfers between devices with their start and end apart: 5, of which 5 were waited for; matrix products, arithmetic and copies ran while one was open for 1% of the time, Pallas kernels for 0%

commit v1 on v0

--- a/solution.py
+++ b/solution.py
@@ -16,7 +16,12 @@
     local_cols = intermediate.shape[1]
     slice_width = local_cols // owner_rows
     own_rows = lax.dynamic_slice_in_dim(amplitudes, layer_index * band_rows, band_rows, 0)
-    all_weights = lax.all_gather(intermediate, "row", axis=0, tiled=True)
+    ring = [intermediate]
+    for hop in range(3):
+        ring.append(lax.ppermute(ring[-1], "row", [(dev, (dev + 1) % 4) for dev in range(4)]))
+    all_weights = jnp.roll(
+        jnp.concatenate(ring[::-1], axis=0), (lax.axis_index("row") + 1) * ring[0].shape[0], axis=0
+    )
     summed = jnp.dot(
         lax.all_gather(own_rows, "col", axis=1, tiled=True),
         all_weights,

time: 154 us -> 137 us (0.89)
  waiting for transfers between devices: 121 us -> 89.9 us
  local copies, waits for them, and re-layouts: 4.12 us -> 16.3 us
  starting transfers between devices: 9.96 us -> 13 us
    all_gather x1 -> x0, waiting for transfers between devices: 82.3 us -> none  [local(): all_weights = lax.all_gather(intermediate, 'row', axis=0, tiled=True)]
    ppermute x0 -> x3, waiting for transfers between devices: none -> 76.3 us  [local(): lax.ppermute(ring[-1], 'row', [(dev, (dev + 1) % 4) for dev in range(4)])]
    all_gather x1, waiting for transfers between devices: 24.8 us -> 0.01 us  [local(): lax.all_gather(own_rows, 'col', axis=1, tiled=True)]
    unnamed x2 -> x11, local copies, waits for them, and re-layouts: 1.22 us -> 12.3 us
    ppermute x0 -> x3, starting transfers between devices: none -> 3.06 us  [local(): lax.ppermute(ring[-1], 'row', [(dev, (dev + 1) % 4) for dev in range(4)])]
  transfers between devices with their start and end apart: 5 -> 7, of which waited for: 5 -> 6; matrix products, arithmetic and copies ran while one was open for 1% -> 11% of each run, Pallas kernels for 0% -> 0%
where the time goes in v1:
time: 137 us
  waiting for transfers between devices  89.9 us (66%)
  local copies, waits for them, and re-layouts  16.3 us (12%)
  between operations  13.4 us (10%)
  starting transfers between devices  13 us (9%)
  matrix products  3.54 us (3%)
    ppermute x3, waiting for transfers between devices, local(): lax.ppermute(ring[-1], 'row', [(dev, (dev + 1) % 4) for dev in range(4)])  76.3 us
    unnamed x11, local copies, waits for them, and re-layouts  12.3 us
    all_to_all x1, waiting for transfers between devices, local(): lax.all_to_all(lax.all_to_all(stacked, 'col', split_axis=0, concat_axis=2...  6.82 us
    dot_general x1, matrix products, local(): jnp.dot(lax.all_gather(own_rows, 'col', axis=1, tiled=True), all_weights,...  3.54 us
    all_to_all x1, waiting for transfers between devices, local(): lax.all_to_all(spread_block, 'col', split_axis=2, concat_axis=1, tiled=True)  3.45 us
    all_to_all x1, starting transfers between devices, local(): lax.all_to_all(lax.all_to_all(stacked, 'col', split_axis=0, concat_axis=2...  3.35 us
    all_to_all x1, waiting for transfers between devices, local(): lax.all_to_all(stacked, 'col', split_axis=0, concat_axis=2, tiled=True)  3.33 us
    all_to_all x1, starting transfers between devices, local(): lax.all_to_all(spread_block, 'col', split_axis=2, concat_axis=1, tiled=True)  3.29 us
  transfers between devices with their start and end apart: 7, of which 6 were waited for; matrix products, arithmetic and copies ran while one was open for 11% of the time, Pallas kernels for 0%

profile of v1, /device:TPU:0, one launch (start us, length us, event | category | flops | bytes accessed | tf_op | source)
XLA Modules:
  0.0 136.8 jit_solution(8312864040941240841)
XLA Ops:
  6.5 0.0 copy-start
  6.5 0.0 all-gather.2.cloned.1.call-start
  6.5 3.1 %collective-permute-start = (bf16[2048,256]{1,0:T(8,128)(2,1)}, bf16[2048,256]{1,0:T(8,128)(2,1)S(1)}, u32[]{:S(2)}, u32[]{:S(2)}) collective-permute-start(bf16[2048,256]{1,0:T(8,128)(2,1)} %param.3), channel_id=1, source_target_pairs={{0,8},{8,16},{16,24},{24,0},{1,9},{9,17},{17,25},{25,1},{2,10},{10... | collective-permute-start | bytes 3145736 | tf_op jit(solution)/shard_map/ppermute | solution.py:21
  9.6 25.4 %collective-permute-done = bf16[2048,256]{1,0:T(8,128)(2,1)S(1)} collective-permute-done((bf16[2048,256]{1,0:T(8,128)(2,1)}, bf16[2048,256]{1,0:T(8,128)(2,1)S(1)}, u32[]{:S(2)}, u32[]{:S(2)}) %collective-permute-start) | collective-permute-done | bytes 1048608 | tf_op jit(solution)/shard_map/ppermute | solution.py:21
  35.0 0.0 collective-permute-start.1
  35.0 0.0 copy-done
  35.0 0.9 constant_dynamic-slice_fusion
  35.9 0.0 all-gather.2.cloned.1.call-update
  35.9 25.3 %collective-permute-done.1 = bf16[2048,256]{1,0:T(8,128)(2,1)} collective-permute-done((bf16[2048,256]{1,0:T(8,128)(2,1)S(1)}, bf16[2048,256]{1,0:T(8,128)(2,1)}, u32[]{:S(2)}, u32[]{:S(2)}) %collective-permute-start.1) | collective-permute-done | bytes 1048608 | tf_op jit(solution)/shard_map/ppermute | solution.py:21
  61.2 0.0 collective-permute-start.2
  61.2 25.6 %collective-permute-done.2 = bf16[2048,256]{1,0:T(8,128)(2,1)} collective-permute-done((bf16[2048,256]{1,0:T(8,128)(2,1)}, bf16[2048,256]{1,0:T(8,128)(2,1)}, u32[]{:S(2)}, u32[]{:S(2)}) %collective-permute-start.2) | collective-permute-done | bytes 1048608 | tf_op jit(solution)/shard_map/ppermute | solution.py:21
  86.8 2.3 %constant_dynamic-update-slice_fusion.7 = bf16[16384,256]{1,0:T(8,128)(2,1)} fusion(bf16[2048,256]{1,0:T(8,128)(2,1)} %collective-permute-done.2), kind=kLoop, calls=%fused_computation.12 | loop fusion | bytes 2097152
  89.1 2.3 %constant_dynamic-update-slice_fusion.6 = bf16[16384,256]{1,0:T(8,128)(2,1)} fusion(bf16[16384,256]{1,0:T(8,128)(2,1)} %constant_dynamic-update-slice_fusion.7, bf16[2048,256]{1,0:T(8,128)(2,1)} %collective-permute-done.1), kind=kLoop, calls=%fused_computation.11 | loop fusion | bytes 2097152
  91.4 1.0 constant_dynamic-update-slice_fusion.5
  92.4 0.0 copy-done.1
  92.4 1.1 constant_dynamic-update-slice_fusion.4
  93.5 2.3 %constant_dynamic-update-slice_fusion.3 = bf16[16384,256]{1,0:T(8,128)(2,1)} fusion(bf16[16384,256]{1,0:T(8,128)(2,1)} %constant_dynamic-update-slice_fusion.4, bf16[2048,256]{1,0:T(8,128)(2,1)} %collective-permute-done.2), kind=kLoop, calls=%fused_computation.8 | loop fusion | bytes 2097152
  95.7 2.3 %constant_dynamic-update-slice_fusion.2 = bf16[16384,256]{1,0:T(8,128)(2,1)} fusion(bf16[16384,256]{1,0:T(8,128)(2,1)} %constant_dynamic-update-slice_fusion.3, bf16[2048,256]{1,0:T(8,128)(2,1)} %collective-permute-done.1), kind=kLoop, calls=%fused_computation.7 | loop fusion | bytes 2097152
  98.0 1.1 constant_dynamic-update-slice_fusion.1
  99.1 1.1 constant_dynamic-update-slice_fusion
  100.2 3.5 %fusion.2 = bf16[128,256]{1,0:T(8,128)(2,1)S(1)} fusion(bf16[128,8192]{1,0:T(8,128)(2,1)} %all-gather.2.cloned.1.call-done, bf16[16384,256]{1,0:T(8,128)(2,1)} %constant_dynamic-update-slice_fusion, s32[]{:T(128)S(6)} %select_n.18), kind=kOutput, calls=%fused_computation.2 | convolution fusion | flops 536903680 | bytes 6356996 | tf_op jit(solution)/shard_map/dot_general | solution.py:25
  103.7 0.6 reshape.21
  104.4 3.3 %all-to-all-start = ((bf16[4,32,2,128]{3,2,1,0:T(2,128)(2,1)}), bf16[4,32,2,128]{3,2,1,0:T(2,128)(2,1)S(1)}, u32[]{:S(2)}, u32[]{:S(2)}) async-start(bf16[4,32,2,128]{3,2,1,0:T(2,128)(2,1)} %reshape.21), calls=%async_computation | async-start | bytes 131072 | tf_op jit(solution)/shard_map/all_to_all | solution.py:37
  107.7 0.1 copy.13
  107.8 0.6 copy.14
  108.4 3.3 %all-to-all-done = bf16[4,32,2,128]{3,2,1,0:T(2,128)(2,1)S(1)} async-done(((bf16[4,32,2,128]{3,2,1,0:T(2,128)(2,1)}), bf16[4,32,2,128]{3,2,1,0:T(2,128)(2,1)S(1)}, u32[]{:S(2)}, u32[]{:S(2)}) %all-to-all-start) | async-done | bytes 65568 | tf_op jit(solution)/shard_map/all_to_all | solution.py:37
  111.7 3.3 %all-to-all-start.2 = ((bf16[128,2,4,32]{0,3,1,2:T(8,128)(2,1)}), bf16[128,2,4,32]{0,3,1,2:T(8,128)(2,1)S(1)}, u32[]{:S(2)}, u32[]{:S(2)}) async-start(bf16[128,2,4,32]{0,3,1,2:T(8,128)(2,1)} %copy.14), calls=%async_computation.2 | async-start | bytes 131072 | tf_op jit(solution)/shard_map/all_to_all | solution.py:32
  115.0 0.6 copy.11
  115.7 3.5 %all-to-all-done.2 = bf16[128,2,4,32]{0,3,1,2:T(8,128)(2,1)S(1)} async-done(((bf16[128,2,4,32]{0,3,1,2:T(8,128)(2,1)}), bf16[128,2,4,32]{0,3,1,2:T(8,128)(2,1)S(1)}, u32[]{:S(2)}, u32[]{:S(2)}) %all-to-all-start.2) | async-done | bytes 65568 | tf_op jit(solution)/shard_map/all_to_all | solution.py:32
  119.1 3.3 %all-to-all-start.1 = ((bf16[1,32,8,128]{3,1,0,2:T(8,128)(2,1)}), bf16[1,32,8,128]{3,1,0,2:T(8,128)(2,1)S(1)}, u32[]{:S(2)}, u32[]{:S(2)}) async-start(bf16[1,32,8,128]{3,1,0,2:T(8,128)(2,1)} %bitcast.2), calls=%async_computation.1 | async-start | bytes 131072 | tf_op jit(solution)/shard_map/all_to_all | solution.py:36
  122.5 6.8 %all-to-all-done.1 = bf16[1,32,8,128]{3,1,0,2:T(8,128)(2,1)S(1)} async-done(((bf16[1,32,8,128]{3,1,0,2:T(8,128)(2,1)}), bf16[1,32,8,128]{3,1,0,2:T(8,128)(2,1)S(1)}, u32[]{:S(2)}, u32[]{:S(2)}) %all-to-all-start.1) | async-done | bytes 65568 | tf_op jit(solution)/shard_map/all_to_all | solution.py:36
  129.3 0.7 bitcast_add_fusion
  (3 shorter events, 0.0 us)
Async XLA Ops:
  6.5 28.5 %copy-start = (bf16[256,2048]{1,0:T(8,128)(2,1)S(1)}, bf16[256,2048]{1,0:T(8,128)(2,1)}, u32[]{:S(2)}) copy-start(bf16[256,2048]{1,0:T(8,128)(2,1)} %param.2) | copy-start | bytes 3145732
  6.5 85.9 %copy-start.1 = (bf16[2048,256]{1,0:T(8,128)(2,1)S(1)}, bf16[2048,256]{1,0:T(8,128)(2,1)}, u32[]{:S(2)}) copy-start(bf16[2048,256]{1,0:T(8,128)(2,1)} %param.3) | copy-start | bytes 3145732
  6.5 93.6 %all-gather.2.cloned.1.call-start = ((), (), s32[]{:S(2)}) async-start(), calls=%async_computation.3 | async-start | bytes 2621440 | tf_op jit(solution)/shard_map/all_gather | solution.py:26
  6.5 28.5 %collective-permute-start = (bf16[2048,256]{1,0:T(8,128)(2,1)}, bf16[2048,256]{1,0:T(8,128)(2,1)S(1)}, u32[]{:S(2)}, u32[]{:S(2)}) collective-permute-start(bf16[2048,256]{1,0:T(8,128)(2,1)} %param.3), channel_id=1, source_target_pairs={{0,8},{8,16},{16,24},{24,0},{1,9},{9,17},{17,25},{25,1},{2,10},{10... | collective-permute-start | bytes 3145736 | tf_op jit(solution)/shard_map/ppermute | solution.py:21
  35.0 26.2 %collective-permute-start.1 = (bf16[2048,256]{1,0:T(8,128)(2,1)S(1)}, bf16[2048,256]{1,0:T(8,128)(2,1)}, u32[]{:S(2)}, u32[]{:S(2)}) collective-permute-start(bf16[2048,256]{1,0:T(8,128)(2,1)S(1)} %collective-permute-done), channel_id=1, source_target_pairs={{0,8},{8,16},{16,24},{24,0},{1,9},{9,17},{17,25},{25,1},{2,10},{10... | collective-permute-start | bytes 3145736 | tf_op jit(solution)/shard_map/ppermute | solution.py:21
  61.2 25.6 %collective-permute-start.2 = (bf16[2048,256]{1,0:T(8,128)(2,1)}, bf16[2048,256]{1,0:T(8,128)(2,1)}, u32[]{:S(2)}, u32[]{:S(2)}) collective-permute-start(bf16[2048,256]{1,0:T(8,128)(2,1)} %collective-permute-done.1), channel_id=1, source_target_pairs={{0,8},{8,16},{16,24},{24,0},{1,9},{9,17},{17,25},{25,1},{2,10},{10... | collective-permute-start | bytes 3145736 | tf_op jit(solution)/shard_map/ppermute | solution.py:21
  104.4 7.4 %all-to-all-start = ((bf16[4,32,2,128]{3,2,1,0:T(2,128)(2,1)}), bf16[4,32,2,128]{3,2,1,0:T(2,128)(2,1)S(1)}, u32[]{:S(2)}, u32[]{:S(2)}) async-start(bf16[4,32,2,128]{3,2,1,0:T(2,128)(2,1)} %reshape.21), calls=%async_computation | async-start | bytes 131072 | tf_op jit(solution)/shard_map/all_to_all | solution.py:37
  111.7 7.4 %all-to-all-start.2 = ((bf16[128,2,4,32]{0,3,1,2:T(8,128)(2,1)}), bf16[128,2,4,32]{0,3,1,2:T(8,128)(2,1)S(1)}, u32[]{:S(2)}, u32[]{:S(2)}) async-start(bf16[128,2,4,32]{0,3,1,2:T(8,128)(2,1)} %copy.14), calls=%async_computation.2 | async-start | bytes 131072 | tf_op jit(solution)/shard_map/all_to_all | solution.py:32
  119.1 10.2 %all-to-all-start.1 = ((bf16[1,32,8,128]{3,1,0,2:T(8,128)(2,1)}), bf16[1,32,8,128]{3,1,0,2:T(8,128)(2,1)S(1)}, u32[]{:S(2)}, u32[]{:S(2)}) async-start(bf16[1,32,8,128]{3,1,0,2:T(8,128)(2,1)} %bitcast.2), calls=%async_computation.1 | async-start | bytes 131072 | tf_op jit(solution)/shard_map/all_to_all | solution.py:36
Sparse Core Ops, SparseCore 0:
  36.0 24.0 all-gather.1
